TPU v7x, 128 devices: a whole 4x4x4 slice. The times are simulated.
128 devices in a mesh: gx: 16 (over y, z), gy: 8 (over x, core).
Axes of the slice: x: 4, y: 4, z: 4, core: 2. Of those that a mesh axis runs over, the one named last changes fastest.
Arguments:
- snapshots: bfloat16 [16, 16, 4, 2048, 512], P('gx', 'gy'), may hold values from -120 to 120
- basis: bfloat16 [16, 16, 4, 24, 2048], P('gx', 'gy'), may hold values from -0.0625 to 0.0625
- node_counts: int32 [16, 16], P('gx', 'gy'), may hold values from 1024 to 2048, as said below
- adjacency: int32 [16, 16, 3], P('gx', 'gy'), may hold values from 0 to 255, as said below
Outputs:
- operator: float32 [16, 16, 397, 24], P('gx', 'gy')
- reduced_states: float32 [16, 16, 24, 512], P('gx', 'gy')
Inputs may be any that keep to these rules, and one draw needn't show every extreme that they name: Node slot n of subdomain g is live iff n < node_counts[g]; at least 1024 slots are live, and one subdomain has all 2048 live. Subdomain (row, col) has id row * 16 + col. Each row of adjacency holds 3 distinct ids other than its own subdomain's, each within one subdomain row and one subdomain column of it.
All inputs are finite; a program needn't handle non-finite values.
Results may differ from a plain program's by a relative error of at most 0.0003.
Values sent between devices are 32-bit elements; how exact they have to be, the bound alone decides.
A program may use at most 64 MiB of HBM per device.

v0:
```python
import jax
import jax.numpy as jnp
from jax import lax
from jax.sharding import Mesh
from jax.sharding import PartitionSpec as P

GX = ("gx_0", "gx_1")
GY = ("gy_0", "gy_1")
GX_GY = ("gx_0", "gx_1", "gy_0", "gy_1")
beta_linear = 0.5
beta_quad = 0.5


def one_axis_at_a_time(x, axes):
    for axis in axes:
        x = lax.psum(x, axis)
    return x


def padded_2(cells, sides, width):
    for axis, dim in sides:
        count = lax.axis_size(axis)
        ends = count - 1
        head = lax.slice_in_dim(cells, 0, width, axis=dim)
        tail = lax.slice_in_dim(cells, cells.shape[dim] - width, cells.shape[dim], axis=dim)
        cells = jnp.concatenate(
            [
                lax.ppermute(tail, axis, [(i, (i + 1) % count) for i in range(ends)]),
                cells,
                lax.ppermute(head, axis, [((i + 1) % count, i) for i in range(ends)]),
            ],
            axis=dim,
        )
    return cells


def build_features(state, near):
    ranks = state.shape[1]
    steps = state.shape[2]
    pieces = [
        jnp.ones((state.shape[0], 1, steps), jnp.float32),
        state,
        near.reshape(state.shape[0], -1, steps),
    ]
    for first in range(ranks):
        pieces.append(state[:, first : first + 1] * state[:, first:])
    return jnp.concatenate(pieces, axis=1)


def pick_rows(pieces, links):
    ids = jnp.arange(pieces.shape[0], dtype=jnp.int32)
    hits = (links[:, :, None] == ids[None, None, :]).astype(jnp.float32)
    return jnp.einsum("sbn,nrk->sbrk", hits, pieces, precision=lax.Precision.HIGHEST)


def solve_one(gram, rhs):
    factor = jnp.linalg.cholesky(gram)
    middle = jax.scipy.linalg.solve_triangular(factor, rhs, lower=True)
    return jax.scipy.linalg.solve_triangular(factor, middle, lower=True, trans=1)


def body(snapshots, basis, node_counts, adjacency):
    values = snapshots[0]
    modes = basis[0]
    counts = node_counts[0]
    links = adjacency[0]
    columns = values.shape[0]
    slots = values.shape[2]
    steps = values.shape[3]
    ranks = modes.shape[2]
    live = jnp.arange(slots, dtype=jnp.int32)[None, :] < counts[:, None]
    masked = modes * live.astype(jnp.bfloat16)[:, None, None, :]
    proj = jnp.einsum("svrp,svpk->svrk", masked, values, preferred_element_type=jnp.float32)
    slotsq = jnp.einsum("svpk,svpk->svp", values, values, preferred_element_type=jnp.float32)
    squares = jnp.sum(slotsq * live.astype(jnp.float32)[:, None, :], axis=(0, 2))
    nodes = jnp.sum(counts.astype(jnp.float32))
    total_subs = lax.axis_size(GX) * lax.axis_size(GY) * columns
    grid_cols = columns * lax.axis_size(GY)
    near_row = links // grid_cols
    near_col = links % grid_cols
    local = (near_row - lax.axis_index(GX) + 1) * (columns + 2) + (
        near_col - lax.axis_index(GY) * columns + 1
    )
    cross = jnp.einsum("svrk,swrk->vw", proj, proj, precision=lax.Precision.HIGHEST)
    sq_all, nodes_all, cross_all = (
        one_axis_at_a_time(squares, GX_GY),
        one_axis_at_a_time(nodes, GX_GY),
        one_axis_at_a_time(cross, GX_GY),
    )
    scale = jnp.sqrt(sq_all / (nodes_all * steps) + 1e-06)
    states = jnp.sum(proj / scale[None, :, None, None], axis=1)
    gnorm = jnp.sum(cross_all / (scale[:, None] * scale[None, :])) / (total_subs * ranks * steps)
    padded = padded_2(states[None], ((GX, 0), (GY, 1)), 1)
    flat = padded.reshape(-1, ranks, steps)
    near = pick_rows(flat, local)
    nbrs = links.shape[1]
    feats = build_features(states, near)
    past = feats[:, :, :-1]
    nlin = 1 + ranks + nbrs * ranks
    nquad = ranks * (ranks + 1) // 2
    reg_diag = steps * jnp.concatenate(
        [
            jnp.full((nlin,), beta_linear, jnp.float32) * gnorm,
            jnp.full((nquad,), beta_quad, jnp.float32) * gnorm * gnorm,
        ]
    )
    gram = (
        jnp.einsum("sfk,sgk->sfg", past, past, precision=lax.Precision.HIGHEST)
        + jnp.diag(reg_diag)[None]
    )
    rhs = jnp.einsum("sfk,srk->sfr", past, states[:, :, 1:], precision=lax.Precision.HIGHEST)
    operator = jax.vmap(solve_one)(gram, rhs)
    return (operator[None], states[None])


def solution(mesh):
    split = Mesh(mesh.devices.reshape(4, 4, 4, 2), ("gx_0", "gx_1", "gy_0", "gy_1"))
    placed = (P(GX, GY, None, None, None), P(GX, GY, None, None, None), P(GX, GY), P(GX, GY, None))
    return jax.shard_map(
        body,
        mesh=split,
        in_specs=placed,
        out_specs=(P(GX, GY, None, None), P(GX, GY, None, None)),
        check_vma=False,
    )
```

profile of v0, /device:TPU:1, one launch (start us, length us, event | category | flops | bytes accessed | tf_op | source)
XLA Modules:
  0.0 333.1 jit_solution(6899208880659183131)
XLA Ops:
  0.6 0.7 fusion.58
  1.4 7.5 %fusion = f32[2,4,2048]{2,1,0:T(4,128)S(1)} fusion(bf16[1,2,4,2048,512]{4,3,2,1,0:T(8,128)(2,1)} %param.4), kind=kLoop, calls=%fused_computation.3 | loop fusion | flops 25149440 | bytes 16842752 | tf_op jit(solution)/shard_map/svpk,svpk->svp/dot_general | solution.py:74
  8.9 3.2 copy-done
  12.0 3.4 %fusion.1 = f32[2,4,24,512]{3,2,1,0:T(8,128)S(1)} fusion(bf16[1,2,4,2048,512]{4,3,2,1,0:T(8,128)(2,1)S(1)} %copy-done, bf16[1,2,4,24,2048]{4,3,2,1,0:T(8,128)(2,1)} %param.5, bf16[2,2048]{1,0:T(2,128)(2,1)S(1)} %get-tuple-element.70), kind=kOutput, calls=%fused_computation.4 | convolution fusion | flops 403046400 | bytes 17965056 | tf_op jit(solution)/shard_map/svrp,svpk->svrk/dot_general | solution.py:73
  15.5 1.9 convolution_bitcast_fusion
  18.1 10.1 %all-reduce.6 = (f32[4]{0:T(128)S(1)}, f32[]{:T(128)}, f32[4,4]{1,0:T(4,128)S(1)}) all-reduce(f32[4]{0:T(128)S(1)} %multiply_reduce_fusion, f32[]{:T(128)} %convert_reduce_fusion, f32[4,4]{1,0:T(4,128)S(1)} %convolution_bitcast_fusion), channel_id=1, replica_groups=mesh['gx_0'=4,'gx_1'=4,'gy_0'=4,'gy_1'=2] {'gx_0'}, use_global_device_ids=true, to_apply=%region_1.0 | all-reduce | flops 21 | bytes 168 | tf_op jit(solution)/shard_map/psum | solution.py:16
  28.3 10.4 %all-reduce.5 = (f32[4]{0:T(128)S(1)}, f32[]{:T(128)}, f32[4,4]{1,0:T(4,128)S(1)}) all-reduce(f32[4]{0:T(128)S(1)} %get-tuple-element.27, f32[]{:T(128)} %get-tuple-element.28, f32[4,4]{1,0:T(4,128)S(1)} %get-tuple-element.29), channel_id=1, replica_groups=mesh['gx_0'=4,'gx_1'=4,'gy_0'=4,'gy_1'=2] {'gx_1'}, use_global_device_ids=true, to_apply=%region_2.3 | all-reduce | flops 21 | bytes 168 | tf_op jit(solution)/shard_map/psum | solution.py:16
  38.6 9.1 %all-reduce.4 = (f32[4]{0:T(128)S(1)}, f32[]{:T(128)}, f32[4,4]{1,0:T(4,128)S(1)}) all-reduce(f32[4]{0:T(128)S(1)} %get-tuple-element.24, f32[]{:T(128)} %get-tuple-element.25, f32[4,4]{1,0:T(4,128)S(1)} %get-tuple-element.26), channel_id=1, replica_groups=mesh['gx_0'=4,'gx_1'=4,'gy_0'=4,'gy_1'=2] {'gy_0'}, use_global_device_ids=true, to_apply=%region_3.4 | all-reduce | flops 21 | bytes 168 | tf_op jit(solution)/shard_map/psum | solution.py:16
  47.7 9.5 %all-reduce.7 = (f32[4]{0:T(128)S(1)}, f32[]{:T(128)}, f32[4,4]{1,0:T(4,128)S(1)}) all-reduce(f32[4]{0:T(128)S(1)} %get-tuple-element.21, f32[]{:T(128)} %get-tuple-element.22, f32[4,4]{1,0:T(4,128)S(1)} %get-tuple-element.23), channel_id=1, replica_groups=mesh['gx_0'=4,'gx_1'=4,'gy_0'=4,'gy_1'=2] {'gy_1'}, use_global_device_ids=true, to_apply=%region_4.5 | all-reduce | flops 21 | bytes 168 | tf_op jit(solution)/shard_map/psum | solution.py:16
  58.0 1.3 collective-permute-start.1
  59.3 4.0 %collective-permute-start = (f32[1,2,24,512]{3,2,1,0:T(8,128)S(1)}, f32[1,2,24,512]{3,2,1,0:T(8,128)S(1)}, u32[]{:S(2)}, u32[]{:S(2)}) collective-permute-start(f32[1,2,24,512]{3,2,1,0:T(8,128)S(1)} %bitcast.156), channel_id=1, source_target_pairs={{0,8},{8,16},{16,24},{24,32},{32,40},{40,48},{48,56},{56,64},{64,7... | collective-permute-start | bytes 294920 | tf_op jit(solution)/shard_map/ppermute | solution.py:28
  63.3 0.6 iota_compare_fusion.4
  63.9 0.7 slice_multiply_fusion.22
  64.6 0.6 pad_convert_fusion
  65.2 0.8 fusion.65
  71.1 0.6 slice_multiply_fusion.17
  71.8 0.6 slice_multiply_fusion.15
  72.9 1.4 fusion.9
  74.9 2.0 collective-permute-start.2
  77.0 2.8 collective-permute-start.3
  80.3 0.8 iota_compare_fusion.2
  81.0 2.4 collective-permute-done.3
  83.5 0.8 fusion.11
  84.3 8.0 %concatenate.48 = f32[2,397,512]{2,1,0:T(8,128)S(1)} concatenate(f32[2,1,512]{2,1,0:T(1,128)S(1)} %broadcast_in_dim.45, f32[2,24,512]{2,1,0:T(8,128)S(1)} %divide_reduce_fusion, f32[2,72,512]{2,1,0:T(8,128)S(1)} %bitcast.161, f32[2,24,512]{2,1,0:T(8,128)S(1)} %broadcast_multiply_fusion, f32[2,23,512]{2,1,0:T(8,128)S(1)} %slice_multiply_fusion.6, ...), dimensions={1} | concatenate | bytes 3252224 | tf_op jit(solution)/shard_map/concatenate | solution.py:47
  92.4 1.5 fusion.5
  93.9 2.8 fusion.7
  96.7 0.7 copy.49
  97.4 2.0 fusion.4
  99.4 1.2 copy-done.2
  100.6 23.5 %custom-call.38 = f32[2,128,128]{2,1,0:T(8,128)S(1)} custom-call(f32[2,128,128]{2,1,0:T(8,128)S(1)} %cholesky.281), custom_call_target="Cholesky" | custom-call | tf_op jit(solution)/shard_map/vmap(jit(cholesky))/cholesky | solution.py:57
  124.1 19.8 %custom-call.39 = f32[2,1,128,128]{2,3,1,0:T(8,128)S(1)} custom-call(f32[2,1,128,128]{3,2,1,0:T(8,128)S(1)} %select_bitcast_fusion.2), custom_call_target="InvertDiagBlocksLowerTriangular" | custom-call | tf_op jit(solution)/shard_map/vmap(jit(cholesky))/cholesky | solution.py:57
  144.2 1.4 constant_dynamic-update-slice_fusion.3
  145.6 1.4 convolution_subtract_fusion
  147.0 23.5 %custom-call.40 = f32[2,128,128]{2,1,0:T(8,128)S(1)} custom-call(f32[2,128,128]{2,1,0:T(8,128)S(1)} %cholesky.285), custom_call_target="Cholesky" | custom-call | tf_op jit(solution)/shard_map/vmap(jit(cholesky))/cholesky | solution.py:57
  170.4 19.7 %custom-call.41 = f32[2,1,128,128]{2,3,1,0:T(8,128)S(1)} custom-call(f32[2,1,128,128]{3,2,1,0:T(8,128)S(1)} %get-tuple-element.39), custom_call_target="InvertDiagBlocksLowerTriangular" | custom-call | tf_op jit(solution)/shard_map/vmap(jit(cholesky))/cholesky | solution.py:57
  190.4 1.3 convolution_subtract_fusion.1
  191.8 23.7 %custom-call.42 = f32[2,128,128]{2,1,0:T(8,128)S(1)} custom-call(f32[2,128,128]{2,1,0:T(8,128)S(1)} %cholesky.290), custom_call_target="Cholesky" | custom-call | tf_op jit(solution)/shard_map/vmap(jit(cholesky))/cholesky | solution.py:57
  215.9 19.7 %custom-call.43 = f32[2,1,128,128]{2,3,1,0:T(8,128)S(1)} custom-call(f32[2,1,128,128]{3,2,1,0:T(8,128)S(1)} %get-tuple-element.37), custom_call_target="InvertDiagBlocksLowerTriangular" | custom-call | tf_op jit(solution)/shard_map/vmap(jit(cholesky))/cholesky | solution.py:57
  235.8 0.9 convolution_subtract_fusion.8
  236.7 2.4 custom-call.44
  239.3 1.3 select_select_fusion
  240.6 7.9 %while.1 = (s32[]{:T(128)}, f32[2,397,397]{2,1,0:T(8,128)S(1)}, s32[3,2]{0,1:T(2,128)S(1)}, f32[3,2,128,128]{3,2,0,1:T(8,128)}, s32[]{:T(128)}) while((s32[]{:T(128)}, f32[2,397,397]{2,1,0:T(8,128)S(1)}, s32[3,2]{0,1:T(2,128)S(1)}, f32[3,2,128,128]{3,2,0,1:T(8,128)}, s32[]{:T(128)}) %tuple.67), condition=%wide.while_cond, body=%wide.while_body.sunk | while | flops 2 | bytes 263277 | solution.py:59
  241.3 2.0 bitcast_dynamic-update-slice_fusion.2
  243.9 2.0 bitcast_dynamic-update-slice_fusion.2
  246.5 2.0 bitcast_dynamic-update-slice_fusion.2
  248.6 1.0 pad_maximum_fusion.1
  249.7 78.6 %custom-call.45 = f32[2,4,128,128]{2,3,1,0:T(8,128)S(1)} custom-call(f32[2,4,128,128]{3,2,1,0:T(8,128)S(1)} %pad_maximum_fusion.1), custom_call_target="InvertDiagBlocksLowerTriangular" | custom-call | tf_op jit(solution)/shard_map/vmap(jit(_solve_triangular))/triangular_solve | solution.py:59
  332.2 0.7 maximum_bitcast_fusion
  (109 shorter events, 12.9 us)
Async XLA Ops:
  1.4 10.7 %copy-start = (bf16[1,2,4,2048,512]{4,3,2,1,0:T(8,128)(2,1)S(1)}, bf16[1,2,4,2048,512]{4,3,2,1,0:T(8,128)(2,1)}, u32[]{:S(2)}) copy-start(bf16[1,2,4,2048,512]{4,3,2,1,0:T(8,128)(2,1)} %param.4) | copy-start | bytes 50331652
  12.0 5.5 %copy-start.7 = (s32[1,2]{1,0:T(1,128)S(1)}, s32[1,2]{1,0:T(1,128)}, u32[]{:S(2)}) copy-start(s32[1,2]{1,0:T(1,128)} %param.6) | copy-start | bytes 28
  58.0 34.4 %copy-start.1 = (f32[2,24,512]{2,1,0:T(8,128)}, f32[2,24,512]{2,1,0:T(8,128)S(1)}, u32[]{:S(2)}) copy-start(f32[2,24,512]{2,1,0:T(8,128)S(1)} %divide_reduce_fusion) | copy-start | bytes 294916
  58.0 16.9 %collective-permute-start.1 = (f32[1,2,24,512]{3,2,1,0:T(8,128)S(1)}, f32[1,2,24,512]{3,2,1,0:T(8,128)S(1)}, u32[]{:S(2)}, u32[]{:S(2)}) collective-permute-start(f32[1,2,24,512]{3,2,1,0:T(8,128)S(1)} %bitcast.155), channel_id=1, source_target_pairs={{8,0},{16,8},{24,16},{32,24},{40,32},{48,40},{56,48},{64,56},{72,6... | collective-permute-start | bytes 294920 | tf_op jit(solution)/shard_map/ppermute | solution.py:30
  59.3 15.6 %collective-permute-start = (f32[1,2,24,512]{3,2,1,0:T(8,128)S(1)}, f32[1,2,24,512]{3,2,1,0:T(8,128)S(1)}, u32[]{:S(2)}, u32[]{:S(2)}) collective-permute-start(f32[1,2,24,512]{3,2,1,0:T(8,128)S(1)} %bitcast.156), channel_id=1, source_target_pairs={{0,8},{8,16},{16,24},{24,32},{32,40},{40,48},{48,56},{56,64},{64,7... | collective-permute-start | bytes 294920 | tf_op jit(solution)/shard_map/ppermute | solution.py:28
  72.6 1.7 copy-start.6
  74.9 6.1 %collective-permute-start.2 = (f32[3,1,24,512]{3,2,1,0:T(8,128)S(1)}, f32[3,1,24,512]{3,2,1,0:T(8,128)S(1)}, u32[]{:S(2)}, u32[]{:S(2)}) collective-permute-start(f32[3,1,24,512]{3,2,1,0:T(8,128)S(1)} %get-tuple-element.35), channel_id=1, source_target_pairs={{0,1},{1,2},{2,3},{3,4},{4,5},{5,6},{6,7},{8,9},{9,10},{10,11},{11... | collective-permute-start | bytes 442376 | tf_op jit(solution)/shard_map/ppermute | solution.py:28
  77.0 6.5 %collective-permute-start.3 = (f32[3,1,24,512]{3,2,1,0:T(8,128)S(1)}, f32[3,1,24,512]{3,2,1,0:T(8,128)S(1)}, u32[]{:S(2)}, u32[]{:S(2)}) collective-permute-start(f32[3,1,24,512]{3,2,1,0:T(8,128)S(1)} %get-tuple-element.36), channel_id=1, source_target_pairs={{1,0},{2,1},{3,2},{4,3},{5,4},{6,5},{7,6},{9,8},{10,9},{11,10},{12... | collective-permute-start | bytes 442376 | tf_op jit(solution)/shard_map/ppermute | solution.py:30
  99.4 1.2 copy-start.2
  145.5 69.9 %copy-start.4 = (pred[128,128]{1,0:T(8,128)(4,1)S(1)}, pred[128,128]{1,0:T(8,128)(4,1)}, u32[]{:S(2)}) copy-start(pred[128,128]{1,0:T(8,128)(4,1)} %get-tuple-element.96) | copy-start | bytes 49156
  146.9 92.1 %copy-start.5 = (pred[13,13]{1,0:T(8,128)(4,1)S(1)}, pred[13,13]{1,0:T(8,128)(4,1)}, u32[]{:S(2)}) copy-start(pred[13,13]{1,0:T(8,128)(4,1)} %iota_compare_fusion.8) | copy-start | bytes 511
  239.2 1.3 copy-start.8
  239.2 9.2 %copy-start.3 = (f32[128,115]{1,0:T(8,128)S(1)}, f32[128,115]{1,0:T(8,128)}, u32[]{:S(2)}) copy-start(f32[128,115]{1,0:T(8,128)} %pad_convert_fusion) | copy-start | bytes 176644
where the time goes:
time: 338 us; the launch traced here: 333 us
  other arithmetic  236 us (70%)
  blocking collectives  39 us (12%)
  local copies, waits for them, and re-layouts  21.6 us (6%)
  matrix products  19.7 us (6%)
  starting transfers between devices  10.1 us (3%)
  between operations  4.2 us (1%)
    another operation x18, other arithmetic, solve_one(): factor = jnp.linalg.cholesky(gram)  134 us
    another operation x8, other arithmetic, solve_one(): jax.scipy.linalg.solve_triangular(factor, middle, lower=True, trans=1)  83 us
    psum x4, blocking collectives, one_axis_at_a_time(): x = lax.psum(x, axis)  39 us
    concatenate x1, local copies, waits for them, and re-layouts, build_features(): return jnp.concatenate(pieces, axis=1)  8.01 us
    another operation x9, local copies, waits for them, and re-layouts  7.89 us
    dot_general x1, other arithmetic, body(): jnp.einsum('svpk,svpk->svp', values, values, preferred_element_type=jnp.f...  7.47 us
  transfers between devices with their start and end apart: 4, of which 1 were waited for; matrix products, arithmetic and copies ran while one was open for 3% of the time, Pallas kernels for 0%

commit v1 on v0

--- a/solution.py
+++ b/solution.py
@@ -13,7 +13,7 @@
 
 def one_axis_at_a_time(x, axes):
     for axis in axes:
-        x = lax.psum(x, axis)
+        x = jnp.sum(lax.all_gather(x, axis), axis=0)
     return x
 
 

time: 338 us -> 393 us (1.16)
  blocking collectives: 39 us -> 70.2 us
  local copies, waits for them, and re-layouts: 21.6 us -> 32.8 us
  matrix products: 19.7 us -> 25 us
    psum x4 -> x0, blocking collectives: 39 us -> none  [one_axis_at_a_time(): x = lax.psum(x, axis)]
    unnamed x0 -> x4, blocking collectives: none -> 36.5 us
    all_gather x0 -> x4, blocking collectives: none -> 33.7 us  [one_axis_at_a_time(): x = jnp.sum(lax.all_gather(x, axis), axis=0)]
    unnamed x30 -> x52, local copies, waits for them, and re-layouts: 4.46 us -> 13 us
    dot_general x1, matrix products: 3.43 us -> 8.1 us  [body(): jnp.einsum('svrp,svpk->svrk', masked, values, preferred_element_type=jnp....]
where the time goes in v1:
time: 393 us; the launch traced here: 386 us
  other arithmetic  239 us (61%)
  blocking collectives  70.2 us (18%)
  local copies, waits for them, and re-layouts  32.8 us (8%)
  matrix products  25 us (6%)
  starting transfers between devices  10.1 us (3%)
  between operations  6.7 us (2%)
    another operation x18, other arithmetic, solve_one(): factor = jnp.linalg.cholesky(gram)  134 us
    another operation x8, other arithmetic, solve_one(): jax.scipy.linalg.solve_triangular(factor, middle, lower=True, trans=1)  81.3 us
    unnamed x4, blocking collectives  36.5 us
    all_gather x4, blocking collectives, one_axis_at_a_time(): x = jnp.sum(lax.all_gather(x, axis), axis=0)  33.7 us
    unnamed x52, local copies, waits for them, and re-layouts  13 us
    concatenate x1, local copies, waits for them, and re-layouts, build_features(): return jnp.concatenate(pieces, axis=1)  10.4 us
    dot_general x1, matrix products, body(): jnp.einsum('svrp,svpk->svrk', masked, values, preferred_element_type=jnp....  8.1 us
  transfers between devices with their start and end apart: 4, of which 1 were waited for; matrix products, arithmetic and copies ran while one was open for 3% of the time, Pallas kernels for 0%

profile of v1, /device:TPU:1, one launch (start us, length us, event | category | flops | bytes accessed | tf_op | source)
XLA Modules:
  0.0 386.3 jit_solution(17392027296718887444)
XLA Ops:
  0.6 1.3 convert_reduce_fusion
  2.0 1.3 dynamic-slice.7
  3.3 1.3 dynamic-slice.6
  5.9 1.3 dynamic-slice.5
  7.7 1.2 dynamic-slice.4
  10.4 7.3 %fusion = f32[2,4,2048]{2,1,0:T(4,128)S(1)} fusion(bf16[1,2,4,2048,512]{4,3,2,1,0:T(8,128)(2,1)} %param.4), kind=kLoop, calls=%fused_computation.3 | loop fusion | flops 25149440 | bytes 16842752 | tf_op jit(solution)/shard_map/svpk,svpk->svp/dot_general | solution.py:74
  17.8 1.4 dynamic-update-slice.27
  19.4 9.5 %all-reduce.14 = (f32[16]{0:T(128)S(1)}, f32[4]{0:T(128)S(1)}) all-reduce(f32[16]{0:T(128)S(1)} %dynamic-update-slice.23, f32[4]{0:T(128)S(1)} %dynamic-update-slice.27), channel_id=2, replica_groups=mesh['gx_0'=4,'gx_1'=4,'gy_0'=4,'gy_1'=2] {'gx_0'}, use_global_device_ids=true, to_apply=%add.4 | all-reduce | flops 20 | bytes 160
  29.7 1.4 dynamic-update-slice.28
  31.2 9.7 %all-reduce.13 = (f32[16]{0:T(128)S(1)}, f32[4]{0:T(128)S(1)}) all-reduce(f32[16]{0:T(128)S(1)} %dynamic-update-slice.24, f32[4]{0:T(128)S(1)} %dynamic-update-slice.28), channel_id=3, replica_groups=mesh['gx_0'=4,'gx_1'=4,'gy_0'=4,'gy_1'=2] {'gx_1'}, use_global_device_ids=true, to_apply=%add.5 | all-reduce | flops 20 | bytes 160
  41.7 1.4 dynamic-update-slice.29
  43.3 8.4 %all-reduce.12 = (f32[16]{0:T(128)S(1)}, f32[4]{0:T(128)S(1)}) all-reduce(f32[16]{0:T(128)S(1)} %dynamic-update-slice.25, f32[4]{0:T(128)S(1)} %dynamic-update-slice.29), channel_id=4, replica_groups=mesh['gx_0'=4,'gx_1'=4,'gy_0'=4,'gy_1'=2] {'gy_0'}, use_global_device_ids=true, to_apply=%add.6 | all-reduce | flops 20 | bytes 160
  52.4 1.4 dynamic-update-slice.30
  54.0 8.8 %all-reduce.15 = (f32[8]{0:T(128)S(1)}, f32[2]{0:T(128)S(1)}) all-reduce(f32[8]{0:T(128)S(1)} %dynamic-update-slice.26, f32[2]{0:T(128)S(1)} %dynamic-update-slice.30), channel_id=5, replica_groups=mesh['gx_0'=4,'gx_1'=4,'gy_0'=4,'gy_1'=2] {'gy_1'}, use_global_device_ids=true, to_apply=%add.7 | all-reduce | flops 10 | bytes 80
  64.3 8.1 %divide_reduce_fusion = (f32[2,24,512]{2,1,0:T(8,128)S(1)}, f32[2,4,24,512]{3,2,1,0:T(8,128)S(1)}) fusion(f32[4]{0:T(128)S(1)} %add_sqrt_fusion, bf16[1,2,4,2048,512]{4,3,2,1,0:T(8,128)(2,1)} %param.4, bf16[1,2,4,24,2048]{4,3,2,1,0:T(8,128)(2,1)S(1)} %copy-done.2, bf16[2,2048]{1,0:T(2,128)(2,1)S(1)} %get-tuple-element.66), kind=kOutput, calls=%fused_computation.38 | convolution fusion | flops 403218432 | bytes 18063376 | tf_op jit(solution)/shard_map/svrp,svpk->svrk/dot_general | solution.py:73
  72.4 1.3 collective-permute-start.1
  73.7 4.0 %collective-permute-start = (f32[1,2,24,512]{3,2,1,0:T(8,128)S(1)}, f32[1,2,24,512]{3,2,1,0:T(8,128)S(1)}, u32[]{:S(2)}, u32[]{:S(2)}) collective-permute-start(f32[1,2,24,512]{3,2,1,0:T(8,128)S(1)} %bitcast.177), channel_id=1, source_target_pairs={{0,8},{8,16},{16,24},{24,32},{32,40},{40,48},{48,56},{56,64},{64,7... | collective-permute-start | bytes 294920 | tf_op jit(solution)/shard_map/ppermute | solution.py:28
  79.6 1.9 convolution_bitcast_fusion
  81.5 8.1 %all-gather.8 = f32[4,4,4]{2,1,0:T(4,128)S(1)} all-gather(f32[1,4,4]{2,1,0:T(4,128)S(1)} %convolution_bitcast_fusion), channel_id=6, replica_groups=mesh['gx_0'=4,'gx_1'=4,'gy_0'=4,'gy_1'=2] {'gx_0'}, dimensions={0}, use_global_device_ids=true | all-gather | bytes 320 | tf_op jit(solution)/shard_map/all_gather | solution.py:16
  89.7 8.1 %all-gather.9 = f32[4,4,4]{2,1,0:T(4,128)S(1)} all-gather(f32[1,4,4]{2,1,0:T(4,128)S(1)} %bitcast.185), channel_id=7, replica_groups=mesh['gx_0'=4,'gx_1'=4,'gy_0'=4,'gy_1'=2] {'gx_1'}, dimensions={0}, use_global_device_ids=true | all-gather | bytes 320 | tf_op jit(solution)/shard_map/all_gather | solution.py:16
  97.8 8.1 %all-gather.10 = f32[4,4,4]{2,1,0:T(4,128)S(1)} all-gather(f32[1,4,4]{2,1,0:T(4,128)S(1)} %bitcast.186), channel_id=8, replica_groups=mesh['gx_0'=4,'gx_1'=4,'gy_0'=4,'gy_1'=2] {'gy_0'}, dimensions={0}, use_global_device_ids=true | all-gather | bytes 320 | tf_op jit(solution)/shard_map/all_gather | solution.py:16
  106.0 9.3 %all-gather.11 = f32[2,4,4]{2,1,0:T(4,128)S(1)} all-gather(f32[1,4,4]{2,1,0:T(4,128)S(1)} %bitcast.187), channel_id=9, replica_groups=mesh['gx_0'=4,'gx_1'=4,'gy_0'=4,'gy_1'=2] {'gy_1'}, dimensions={0}, use_global_device_ids=true | all-gather | bytes 192 | tf_op jit(solution)/shard_map/all_gather | solution.py:16
  123.9 1.4 fusion.9
  126.0 1.9 collective-permute-start.2
  127.9 2.9 collective-permute-start.3
  131.4 3.0 collective-permute-done.3
  135.3 10.4 %concatenate.48 = f32[2,397,512]{2,1,0:T(8,128)S(1)} concatenate(f32[2,1,512]{2,1,0:T(1,128)S(1)} %broadcast_in_dim.45, f32[2,24,512]{2,1,0:T(8,128)S(1)} %get-tuple-element.67, f32[2,72,512]{2,1,0:T(8,128)S(1)} %bitcast.182, f32[2,24,512]{2,1,0:T(8,128)S(1)} %broadcast_multiply_fusion, f32[2,23,512]{2,1,0:T(8,128)S(1)} %slice_multiply_fusion.6, ...), dimensions={1} | concatenate | bytes 3252224 | tf_op jit(solution)/shard_map/concatenate | solution.py:47
  145.7 2.2 fusion.5
  147.9 2.8 fusion.7
  151.4 2.0 fusion.4
  153.4 1.2 copy-done.1
  154.6 23.5 %custom-call.38 = f32[2,128,128]{2,1,0:T(8,128)S(1)} custom-call(f32[2,128,128]{2,1,0:T(8,128)S(1)} %cholesky.281), custom_call_target="Cholesky" | custom-call | tf_op jit(solution)/shard_map/vmap(jit(cholesky))/cholesky | solution.py:57
  178.1 19.8 %custom-call.39 = f32[2,1,128,128]{2,3,1,0:T(8,128)S(1)} custom-call(f32[2,1,128,128]{3,2,1,0:T(8,128)S(1)} %select_bitcast_fusion.2), custom_call_target="InvertDiagBlocksLowerTriangular" | custom-call | tf_op jit(solution)/shard_map/vmap(jit(cholesky))/cholesky | solution.py:57
  198.2 1.4 constant_dynamic-update-slice_fusion.3
  199.6 1.4 convolution_subtract_fusion
  201.0 23.5 %custom-call.40 = f32[2,128,128]{2,1,0:T(8,128)S(1)} custom-call(f32[2,128,128]{2,1,0:T(8,128)S(1)} %cholesky.285), custom_call_target="Cholesky" | custom-call | tf_op jit(solution)/shard_map/vmap(jit(cholesky))/cholesky | solution.py:57
  224.5 19.7 %custom-call.41 = f32[2,1,128,128]{2,3,1,0:T(8,128)S(1)} custom-call(f32[2,1,128,128]{3,2,1,0:T(8,128)S(1)} %get-tuple-element.35), custom_call_target="InvertDiagBlocksLowerTriangular" | custom-call | tf_op jit(solution)/shard_map/vmap(jit(cholesky))/cholesky | solution.py:57
  244.4 1.3 convolution_subtract_fusion.1
  245.8 23.7 %custom-call.42 = f32[2,128,128]{2,1,0:T(8,128)S(1)} custom-call(f32[2,128,128]{2,1,0:T(8,128)S(1)} %cholesky.290), custom_call_target="Cholesky" | custom-call | tf_op jit(solution)/shard_map/vmap(jit(cholesky))/cholesky | solution.py:57
  269.9 19.7 %custom-call.43 = f32[2,1,128,128]{2,3,1,0:T(8,128)S(1)} custom-call(f32[2,1,128,128]{3,2,1,0:T(8,128)S(1)} %get-tuple-element.33), custom_call_target="InvertDiagBlocksLowerTriangular" | custom-call | tf_op jit(solution)/shard_map/vmap(jit(cholesky))/cholesky | solution.py:57
  289.8 0.9 convolution_subtract_fusion.8
  290.7 2.4 custom-call.44
  293.9 7.8 %while.1 = (s32[]{:T(128)}, f32[2,397,397]{2,1,0:T(8,128)S(1)}, s32[3,2]{0,1:T(2,128)S(1)}, f32[3,2,128,128]{3,2,0,1:T(8,128)}, s32[]{:T(128)}) while((s32[]{:T(128)}, f32[2,397,397]{2,1,0:T(8,128)S(1)}, s32[3,2]{0,1:T(2,128)S(1)}, f32[3,2,128,128]{3,2,0,1:T(8,128)}, s32[]{:T(128)}) %tuple.68), condition=%wide.while_cond, body=%wide.while_body.sunk | while | flops 2 | bytes 263277 | solution.py:59
  294.5 2.0 bitcast_dynamic-update-slice_fusion.2
  297.1 2.0 bitcast_dynamic-update-slice_fusion.2
  299.7 2.0 bitcast_dynamic-update-slice_fusion.2
  301.8 1.0 pad_maximum_fusion.1
  302.8 78.6 %custom-call.45 = f32[2,4,128,128]{2,3,1,0:T(8,128)S(1)} custom-call(f32[2,4,128,128]{3,2,1,0:T(8,128)S(1)} %pad_maximum_fusion.1), custom_call_target="InvertDiagBlocksLowerTriangular" | custom-call | tf_op jit(solution)/shard_map/vmap(jit(_solve_triangular))/triangular_solve | solution.py:59
  (150 shorter events, 24.3 us)
Async XLA Ops:
  10.4 53.9 %copy-start.2 = (bf16[1,2,4,24,2048]{4,3,2,1,0:T(8,128)(2,1)S(1)}, bf16[1,2,4,24,2048]{4,3,2,1,0:T(8,128)(2,1)}, u32[]{:S(2)}) copy-start(bf16[1,2,4,24,2048]{4,3,2,1,0:T(8,128)(2,1)} %param.5) | copy-start | bytes 2359300
  72.4 73.3 %copy-start = (f32[2,24,512]{2,1,0:T(8,128)}, f32[2,24,512]{2,1,0:T(8,128)S(1)}, u32[]{:S(2)}) copy-start(f32[2,24,512]{2,1,0:T(8,128)S(1)} %get-tuple-element.67) | copy-start | bytes 294916
  72.4 53.5 %collective-permute-start.1 = (f32[1,2,24,512]{3,2,1,0:T(8,128)S(1)}, f32[1,2,24,512]{3,2,1,0:T(8,128)S(1)}, u32[]{:S(2)}, u32[]{:S(2)}) collective-permute-start(f32[1,2,24,512]{3,2,1,0:T(8,128)S(1)} %bitcast.176), channel_id=1, source_target_pairs={{8,0},{16,8},{24,16},{32,24},{40,32},{48,40},{56,48},{64,56},{72,6... | collective-permute-start | bytes 294920 | tf_op jit(solution)/shard_map/ppermute | solution.py:30
  73.7 52.2 %collective-permute-start = (f32[1,2,24,512]{3,2,1,0:T(8,128)S(1)}, f32[1,2,24,512]{3,2,1,0:T(8,128)S(1)}, u32[]{:S(2)}, u32[]{:S(2)}) collective-permute-start(f32[1,2,24,512]{3,2,1,0:T(8,128)S(1)} %bitcast.177), channel_id=1, source_target_pairs={{0,8},{8,16},{16,24},{24,32},{32,40},{40,48},{48,56},{56,64},{64,7... | collective-permute-start | bytes 294920 | tf_op jit(solution)/shard_map/ppermute | solution.py:28
  123.7 1.6 copy-start.8
  126.0 5.4 %collective-permute-start.2 = (f32[3,1,24,512]{3,2,1,0:T(8,128)S(1)}, f32[3,1,24,512]{3,2,1,0:T(8,128)S(1)}, u32[]{:S(2)}, u32[]{:S(2)}) collective-permute-start(f32[3,1,24,512]{3,2,1,0:T(8,128)S(1)} %get-tuple-element.31), channel_id=1, source_target_pairs={{0,1},{1,2},{2,3},{3,4},{4,5},{5,6},{6,7},{8,9},{9,10},{10,11},{11... | collective-permute-start | bytes 442376 | tf_op jit(solution)/shard_map/ppermute | solution.py:28
  127.9 6.5 %collective-permute-start.3 = (f32[3,1,24,512]{3,2,1,0:T(8,128)S(1)}, f32[3,1,24,512]{3,2,1,0:T(8,128)S(1)}, u32[]{:S(2)}, u32[]{:S(2)}) collective-permute-start(f32[3,1,24,512]{3,2,1,0:T(8,128)S(1)} %get-tuple-element.32), channel_id=1, source_target_pairs={{1,0},{2,1},{3,2},{4,3},{5,4},{6,5},{7,6},{9,8},{10,9},{11,10},{12... | collective-permute-start | bytes 442376 | tf_op jit(solution)/shard_map/ppermute | solution.py:30
  151.4 26.7 %copy-start.5 = (pred[128,128]{1,0:T(8,128)(4,1)S(1)}, pred[128,128]{1,0:T(8,128)(4,1)}, u32[]{:S(2)}) copy-start(pred[128,128]{1,0:T(8,128)(4,1)} %get-tuple-element.93) | copy-start | bytes 49156
  153.4 1.2 copy-start.1
  199.6 69.9 %copy-start.6 = (pred[128,128]{1,0:T(8,128)(4,1)S(1)}, pred[128,128]{1,0:T(8,128)(4,1)}, u32[]{:S(2)}) copy-start(pred[128,128]{1,0:T(8,128)(4,1)} %get-tuple-element.94) | copy-start | bytes 49156
  200.9 92.1 %copy-start.7 = (pred[13,13]{1,0:T(8,128)(4,1)S(1)}, pred[13,13]{1,0:T(8,128)(4,1)}, u32[]{:S(2)}) copy-start(pred[13,13]{1,0:T(8,128)(4,1)} %iota_compare_fusion.8) | copy-start | bytes 511
  293.2 0.6 copy-start.9
  293.3 8.4 %copy-start.4 = (f32[128,115]{1,0:T(8,128)S(1)}, f32[128,115]{1,0:T(8,128)}, u32[]{:S(2)}) copy-start(f32[128,115]{1,0:T(8,128)} %pad_convert_fusion) | copy-start | bytes 176644
  293.6 87.9 %copy-start.3 = (f32[2,397,24]{1,2,0:T(8,128)S(1)}, f32[2,397,24]{1,2,0:T(8,128)}, u32[]{:S(2)}) copy-start(f32[2,397,24]{1,2,0:T(8,128)} %fusion.5) | copy-start | bytes 228676
